TPU v7x, 16 devices: a 4x2x1 block of a 4x4x8 slice. The times are simulated.
16 devices in a mesh: dp: 2 (over y, z), ep: 8 (over x, core).
Axes of the slice: x: 4, y: 2, z: 1, core: 2. Of those that a mesh axis runs over, the one named last changes fastest.
The devices are a block of a 4x4x8 slice.
Arguments:
- tokens: bfloat16 [8192, 2048], P(('dp', 'ep')), parts along dimension 0
- expert_ids: int32 [8192, 6], P(('dp', 'ep')), parts along dimension 0
- gate_vals: float32 [8192, 6], P(('dp', 'ep')), parts along dimension 0
- slots: int32 [8192, 6], P(('dp', 'ep')), parts along dimension 0
- shared_w1: bfloat16 [2048, 2816], replicated
- shared_w3: bfloat16 [2048, 2816], replicated
- shared_w2: bfloat16 [2816, 2048], replicated
- shared_gate: bfloat16 [2048], replicated
- expert_w1: bfloat16 [64, 2048, 1408], P('ep')
- expert_w3: bfloat16 [64, 2048, 1408], P('ep')
- expert_w2: bfloat16 [64, 1408, 2048], P('ep')
Outputs:
- output: bfloat16 [8192, 2048], P(('dp', 'ep')), parts along dimension 0
There are 2 independent parts. A program takes and returns all parts, laid end to end along the dimension named above; an argument that names none is the same for every part.
All inputs are finite; a program needn't handle non-finite values.
Results may differ from a plain program's by a relative error of at most 0.00518217.
Values are sent between devices in bfloat16 or wider.
A program may use at most 768 MiB of HBM per device.

v0:
```python
import jax
import jax.numpy as jnp
from jax import lax
from jax.sharding import PartitionSpec as P


def solution(mesh):
    num_ep = mesh.shape['ep']
    row_spec = P(('dp', 'ep'), None)
    replicated = P()
    expert_spec = P('ep', None, None)

    def device_step(tokens, expert_ids, gate_vals, slots, shared_w1, shared_w3, shared_w2, shared_gate, expert_w1, expert_w3, expert_w2):
        tok_count, hidden = tokens.shape
        top_k = expert_ids.shape[1]
        local_experts = expert_w1.shape[0]
        num_experts = local_experts * num_ep
        capacity = 8 * ((2 * tok_count * top_k + 8 * num_experts - 1) // (8 * num_experts))
        buf_rows = num_experts * capacity
        kept_mask = slots >= 0
        slot_dest = jnp.where(kept_mask, expert_ids * capacity + slots, buf_rows)
        copy_tok = jnp.arange(tok_count * top_k, dtype=jnp.int32) // top_k
        row_owner = jnp.full((buf_rows + 1,), tok_count, jnp.int32).at[slot_dest.reshape(-1)].set(copy_tok)
        send_buf = jnp.take(tokens, row_owner[:buf_rows], axis=0, mode='fill', fill_value=0)
        recv_buf = lax.all_to_all(send_buf.reshape(num_ep, local_experts * capacity, hidden), 'ep', 0, 0, tiled=True)
        expert_in = recv_buf.reshape(num_ep, local_experts, capacity, hidden)
        act_a = jnp.einsum('secd,edf->secf', expert_in, expert_w1, preferred_element_type=jnp.float32)
        act_b = jnp.einsum('secd,edf->secf', expert_in, expert_w3, preferred_element_type=jnp.float32)
        hidden_act = (jax.nn.silu(act_a) * act_b).astype(jnp.bfloat16)
        expert_out = jnp.einsum('secf,efd->secd', hidden_act, expert_w2, preferred_element_type=jnp.float32).astype(jnp.bfloat16)
        back_buf = lax.all_to_all(expert_out.reshape(num_ep, local_experts * capacity, hidden), 'ep', 0, 0, tiled=True)
        picked = jnp.take(back_buf.reshape(buf_rows, hidden), slot_dest, axis=0, mode='fill', fill_value=0)
        weights = jnp.where(kept_mask, gate_vals, 0.0)[:, :, None]
        routed = jnp.sum(weights * picked, axis=1)
        gate_logit = jnp.dot(tokens, shared_gate, preferred_element_type=jnp.float32)
        shared_a = jnp.dot(tokens, shared_w1, preferred_element_type=jnp.float32)
        shared_b = jnp.dot(tokens, shared_w3, preferred_element_type=jnp.float32)
        shared_h = (jax.nn.silu(shared_a) * shared_b).astype(jnp.bfloat16)
        shared_out = jnp.dot(shared_h, shared_w2, preferred_element_type=jnp.float32)
        total = tokens.astype(jnp.float32) + jax.nn.sigmoid(gate_logit)[:, None] * shared_out + routed
        return total.astype(jnp.bfloat16)

    return jax.shard_map(device_step, mesh=mesh, in_specs=(row_spec, row_spec, row_spec, row_spec, replicated, replicated, replicated, replicated, expert_spec, expert_spec, expert_spec), out_specs=row_spec, check_vma=False)
```

profile of v0, /device:TPU:112, one launch (start us, length us, event | category | flops | bytes accessed | tf_op | source)
XLA Modules:
  0.0 913.3 jit_solution(945135000760672847)
XLA Ops:
  0.0 1.3 compare_and_fusion.1
  1.4 0.1 copy.16
  1.5 0.2 reshape.60
  1.7 11.8 %scatter_custom_fusion = s32[6145]{0:T(1024)S(1)} fusion(s32[3072]{0:T(1024)S(1)} %bitcast.65, s32[3072]{0:T(1024)S(1)} %add_select_fusion, s32[]{:T(128)} %constant.39.clone.1), kind=kCustom, calls=%fused_computation.35 | custom fusion | bytes 24584 | tf_op jit(solution)/shard_map/scatter | solution.py:23
  13.6 48.2 %gather_fusion = bf16[6144,2048]{1,0:T(8,128)(2,1)} fusion(bf16[512,2048]{1,0:T(8,128)(2,1)} %param.11, s32[6144]{0:T(1024)S(1)} %get-tuple-element.8), kind=kCustom, calls=%fused_computation | custom fusion | bytes 50356224 | tf_op jit(solution)/shard_map/jit(_take)/gather | solution.py:24
  61.8 0.0 copy-done.1
  61.9 12.3 %broadcast_select_fusion = bf16[8,768,2048]{2,1,0:T(8,128)(2,1)S(1)} fusion(bf16[8,768,2048]{2,1,0:T(8,128)(2,1)} %bitcast.62, pred[8,768]{1,0:T(8,128)(4,1)S(1)} %compare_and_fusion), kind=kLoop, calls=%fused_computation.18 | loop fusion | flops 12582912 | bytes 50337792 | tf_op jit(solution)/shard_map/jit(_take)/select_n | solution.py:24
  74.1 279.9 %all_to_all.10 = bf16[8,768,2048]{2,1,0:T(8,128)(2,1)} all-to-all(bf16[8,768,2048]{2,1,0:T(8,128)(2,1)S(1)} %broadcast_select_fusion), channel_id=1, replica_groups=mesh['dp'=2,'ep'=8] {'ep'}, dimensions={0} | all-to-all | bytes 50331648 | tf_op jit(solution)/shard_map/all_to_all | solution.py:25
  354.0 49.1 %fusion.2 = f32[8,8,96,1408]{3,2,1,0:T(8,128)} fusion(bf16[8,2048,1408]{2,1,0:T(8,128)(2,1)} %param.20, bf16[8,8,96,2048]{3,2,1,0:T(8,128)(2,1)} %bitcast.63), kind=kOutput, calls=%fused_computation.5 | convolution fusion | flops 35433480192 | bytes 105906176 | tf_op jit(solution)/shard_map/secd,edf->secf/dot_general | solution.py:28
  403.1 58.6 %fusion.6 = bf16[8,8,96,1408]{3,2,0,1:T(8,128)(2,1)} fusion(f32[8,8,96,1408]{3,2,1,0:T(8,128)} %fusion.2, bf16[8,2048,1408]{2,1,0:T(8,128)(2,1)} %param.19, bf16[8,8,96,2048]{3,2,1,0:T(8,128)(2,1)} %bitcast.64), kind=kOutput, calls=%fused_computation.10 | convolution fusion | flops 35485384704 | bytes 123207680 | tf_op jit(solution)/shard_map/secd,edf->secf/dot_general | solution.py:27
  461.7 48.3 %convert_bitcast_fusion = bf16[8,8,96,2048]{3,2,0,1:T(8,128)(2,1)} fusion(bf16[8,8,96,1408]{3,2,0,1:T(8,128)(2,1)} %fusion.6, bf16[8,1408,2048]{2,1,0:T(8,128)(2,1)} %param.21), kind=kOutput, calls=%fused_computation.17 | convolution fusion | flops 35446063104 | bytes 88604672 | tf_op jit(solution)/shard_map/secf,efd->secd/dot_general | solution.py:30
  510.1 21.0 %copy.18 = bf16[8,8,96,2048]{3,2,1,0:T(8,128)(2,1)} copy(bf16[8,8,96,2048]{3,2,0,1:T(8,128)(2,1)} %convert_bitcast_fusion) | data formatting | bytes 50331648 | tf_op jit(solution)/shard_map/convert_element_type | solution.py:30
  531.1 0.0 copy-start.6
  531.1 0.0 copy-start
  531.1 6.9 all-to-all-start.1
  538.0 0.0 copy-done.2
  538.0 0.1 copy.19
  538.2 0.2 reshape.74
  538.4 0.0 copy-done.5
  538.4 0.2 copy.15
  538.6 0.0 copy-done.3
  538.6 0.0 copy-done.4
  538.6 0.1 copy.14
  538.8 0.0 copy-done.6
  538.8 0.0 copy-done
  538.8 0.6 fusion.23
  539.5 11.1 %fusion.24 = f32[512,2816]{1,0:T(8,128)} fusion(bf16[512,2048]{1,0:T(8,128)(2,1)S(1)} %copy-done, bf16[2048,2816]{1,0:T(8,128)(2,1)} %param.15), kind=kOutput, calls=%fused_computation.46 | convolution fusion | flops 5905580032 | bytes 19398656 | tf_op jit(solution)/shard_map/dot_general | solution.py:36
  550.6 261.6 %all-to-all-done.1 = bf16[8,768,2048]{2,1,0:T(8,128)(2,1)} async-done(((bf16[8,768,2048]{2,1,0:T(8,128)(2,1)}), bf16[8,768,2048]{2,1,0:T(8,128)(2,1)}, u32[]{:S(2)}, u32[]{:S(2)}) %all-to-all-start.1) | async-done | bytes 25165856 | tf_op jit(solution)/shard_map/all_to_all | solution.py:31
  812.2 35.2 %gather_fusion.1 = bf16[3072,2048]{1,0:T(8,128)(2,1)} fusion(bf16[6144,2048]{1,0:T(8,128)(2,1)} %bitcast.14, s32[3072]{0:T(1024)S(1)} %broadcast_clamp_fusion), kind=kCustom, calls=%fused_computation.1 | custom fusion | bytes 25178112 | tf_op jit(solution)/shard_map/jit(_take)/gather | solution.py:32
  847.4 20.4 %reshape.73 = bf16[512,6,2048]{2,1,0:T(8,128)(2,1)} reshape(bf16[3072,2048]{1,0:T(8,128)(2,1)} %gather_fusion.1) | data formatting | bytes 25165824 | tf_op jit(solution)/shard_map/jit(_take)/gather | solution.py:32
  867.8 21.2 %multiply_reduce_fusion = f32[512,2048]{1,0:T(8,128)} fusion(bf16[512,6,2048]{2,1,0:T(8,128)(2,1)} %reshape.73, f32[512,6]{1,0:T(8,128)S(1)} %copy.14, pred[512,6]{1,0:T(8,128)(4,1)S(1)} %copy.15), kind=kLoop, calls=%fused_computation.16 | loop fusion | flops 24117248 | bytes 16792576 | tf_op jit(solution)/shard_map/reduce_sum | solution.py:34
  889.0 24.0 %add_convert_fusion = bf16[512,2048]{1,0:T(8,128)(2,1)} fusion(f32[512,2048]{1,0:T(8,128)} %multiply_reduce_fusion, bf16[512,2048]{1,0:T(8,128)(2,1)S(1)} %copy-done, bf16[2816,2048]{1,0:T(8,128)(2,1)} %param.17, f32[512]{0:T(512)S(1)} %add_divide_fusion, f32[512,2816]{1,0:T(8,128)} %fusion.24, bf16[2048,2816]{1,0:T(8,128)(2,1)} %param.16), kind=kOutput, calls=%fused_computation.22 | convolution fusion | flops 11825053696 | bytes 37226496 | tf_op jit(solution)/shard_map/dot_general | solution.py:39
  (15 shorter events, 0.1 us)
Async XLA Ops:
  1.4 60.5 %copy-start.1 = (s32[512,6]{0,1:T(8,128)}, s32[512,6]{0,1:T(8,128)S(1)}, u32[]{:S(2)}) copy-start(s32[512,6]{0,1:T(8,128)S(1)} %get-tuple-element.6) | copy-start | bytes 36868
  531.1 7.0 copy-start.2
  531.1 7.3 copy-start.5
  531.1 7.5 copy-start.3
  531.1 7.5 copy-start.4
  531.1 7.7 copy-start.6
  531.1 7.7 copy-start
  531.1 281.1 %all-to-all-start.1 = ((bf16[8,768,2048]{2,1,0:T(8,128)(2,1)}), bf16[8,768,2048]{2,1,0:T(8,128)(2,1)}, u32[]{:S(2)}, u32[]{:S(2)}) async-start(bf16[8,768,2048]{2,1,0:T(8,128)(2,1)} %bitcast.61), calls=%async_computation.1 | async-start | bytes 50331648 | tf_op jit(solution)/shard_map/all_to_all | solution.py:31
where the time goes:
time: 917 us; the launch traced here: 913 us
  blocking collectives  280 us (31%)
  waiting for transfers between devices  262 us (29%)
  matrix products  192 us (21%)
  local copies, waits for them, and re-layouts  138 us (15%)
  other arithmetic  34.9 us (4%)
    all_to_all x1, blocking collectives, device_step(): lax.all_to_all(send_buf.reshape(num_ep, local_experts * capacity, hidden)...  280 us
    all_to_all x1, waiting for transfers between devices, device_step(): lax.all_to_all(expert_out.reshape(num_ep, local_experts * capacity, hidde...  262 us
    dot_general x1, matrix products, device_step(): jnp.einsum('secd,edf->secf', expert_in, expert_w1, preferred_element_type...  58.6 us
    gather x2, local copies, waits for them, and re-layouts, device_step(): jnp.take(back_buf.reshape(buf_rows, hidden), slot_dest, axis=0, mode='fil...  55.6 us
    dot_general x1, matrix products, device_step(): jnp.einsum('secd,edf->secf', expert_in, expert_w3, preferred_element_type...  49.1 us
    dot_general x1, matrix products, device_step(): jnp.einsum('secf,efd->secd', hidden_act, expert_w2, preferred_element_typ...  48.3 us
    gather x1, local copies, waits for them, and re-layouts, device_step(): jnp.take(tokens, row_owner[:buf_rows], axis=0, mode='fill', fill_value=0)  48.2 us
    dot_general x1, matrix products, device_step(): jnp.dot(shared_h, shared_w2, preferred_element_type=jnp.float32)  24 us
  transfers between devices with their start and end apart: 1, of which 1 were waited for; matrix products, arithmetic and copies ran while one was open for 1% of the time, Pallas kernels for 0%

commit v1 on v0

v1 whole, which is shorter than its diff:
```python
import functools

import jax
import jax.numpy as jnp
from jax import lax
from jax.experimental import pallas as pl
from jax.experimental.pallas import tpu as pltpu
from jax.sharding import PartitionSpec as P

LANES = 128
TILE = 128
LOW = 32
VMEM_BYTES = 67043328


def chunk_sizes(tok_count):
    quarter = tok_count // 4
    return (quarter, quarter, quarter, quarter)


def router_kernel(sizes, top_k, meta_ref, me_ref, tok_ref, gate_ref, cnt_ref, rank_ref, g_ref):
    num_src = meta_ref.shape[0]
    num_e = rank_ref.shape[0]
    highs = tok_ref.shape[2]
    first = (me_ref[0] * num_e).astype(jnp.float32)
    e_idx = lax.broadcasted_iota(jnp.int32, (num_e, LANES), 0).astype(jnp.float32) + first
    upper = (lax.broadcasted_iota(jnp.int32, (LANES, LANES), 0)
             < lax.broadcasted_iota(jnp.int32, (LANES, LANES), 1)).astype(jnp.float32).astype(jnp.bfloat16)
    start = 0
    for c, size in enumerate(sizes):
        total = num_src * size
        carry = jnp.zeros((num_e, 1), jnp.float32)
        for s in range(num_src):
            for b in range(size // LANES):
                lane0 = start + b * LANES
                mask = jnp.zeros((num_e, LANES), jnp.float32)
                gate = jnp.zeros((num_e, LANES), jnp.float32)
                for k in range(top_k):
                    hit = meta_ref[s, k:k + 1, lane0:lane0 + LANES] == e_idx
                    mask = mask + jnp.where(hit, 1.0, 0.0)
                    gate = gate + jnp.where(hit, meta_ref[s, top_k + k:top_k + k + 1, lane0:lane0 + LANES], 0.0)
                rank = jnp.dot(mask.astype(jnp.bfloat16), upper, preferred_element_type=jnp.float32) + carry
                carry = carry + jnp.sum(mask, axis=1, keepdims=True)
                col = s * size + b * LANES
                rank_ref[:, col:col + LANES] = jnp.where(mask > 0.5, rank, -1.0)
                g_ref[:, col:col + LANES] = gate
        cnt_ref[c] = jnp.broadcast_to(carry, (num_e, LANES)).astype(jnp.int32)
        pos = lax.broadcasted_iota(jnp.int32, (1, total), 1)
        pos_hi = (pos // 64).astype(jnp.float32)
        pos_lo = (pos % 64).astype(jnp.float32)
        hi_iota = lax.broadcasted_iota(jnp.int32, (highs, total), 0).astype(jnp.float32)
        lo_iota = lax.broadcasted_iota(jnp.int32, (LOW, total), 0).astype(jnp.float32)
        slot_iota = (lax.broadcasted_iota(jnp.int32, (highs, LOW), 0) * LOW
                     + lax.broadcasted_iota(jnp.int32, (highs, LOW), 1)).astype(jnp.float32)
        for e in range(num_e):
            rank = rank_ref[e:e + 1, 0:total]
            gate = g_ref[e:e + 1, 0:total]
            hi = jnp.floor(rank * (1.0 / LOW))
            lo = rank - hi * LOW
            in_hi = hi_iota == hi
            in_lo = (lo_iota == lo).astype(jnp.float32).astype(jnp.bfloat16)
            gate_a = gate.astype(jnp.bfloat16).astype(jnp.float32)
            rest = gate - gate_a
            gate_b = rest.astype(jnp.bfloat16).astype(jnp.float32)
            gate_c = rest - gate_b
            left = jnp.concatenate(
                [jnp.where(in_hi, v, 0.0) for v in (pos_hi, pos_lo, gate_a, gate_b, gate_c)], axis=0)
            table = lax.dot_general(left.astype(jnp.bfloat16), in_lo, (((1,), (1,)), ((), ())),
                                    preferred_element_type=jnp.float32)
            tok = table[0:highs] * 64.0 + table[highs:2 * highs]
            live = slot_iota < carry[e:e + 1, 0:1]
            tok_ref[c, e] = jnp.where(live, tok, float(total)).astype(jnp.int32)
            gate_ref[c, e] = table[2 * highs:3 * highs] + (table[3 * highs:4 * highs] + table[4 * highs:5 * highs])
        start += size


def route(meta_all, me, sizes, top_k, num_e, rows_max):
    num_src = meta_all.shape[0]
    n_chunks = len(sizes)
    highs = rows_max // LOW
    width = num_src * max(sizes)
    tok, gate, cnt = pl.pallas_call(
        functools.partial(router_kernel, sizes, top_k),
        out_shape=(jax.ShapeDtypeStruct((n_chunks, num_e, highs, LOW), jnp.int32),
                   jax.ShapeDtypeStruct((n_chunks, num_e, highs, LOW), jnp.float32),
                   jax.ShapeDtypeStruct((n_chunks, num_e, LANES), jnp.int32)),
        in_specs=[pl.BlockSpec(memory_space=pltpu.VMEM), pl.BlockSpec(memory_space=pltpu.SMEM)],
        out_specs=(pl.BlockSpec(memory_space=pltpu.VMEM),) * 3,
        scratch_shapes=[pltpu.VMEM((num_e, width), jnp.float32), pltpu.VMEM((num_e, width), jnp.float32)],
        compiler_params=pltpu.CompilerParams(vmem_limit_bytes=32 * 1024 * 1024),
        name="router",
    )(meta_all, me)
    return (tok.reshape(n_chunks, num_e, rows_max), gate.reshape(n_chunks, num_e, rows_max), cnt[:, :, 0])


def ffn_kernel(cnt_ref, tok_ref, gate_ref, x_hbm, w1_ref, w3_ref, w2_ref, out_hbm,
               stage, xf, yf, xg, hb, rg, in_sem, out_sem):
    e = pl.program_id(0)
    num_e = pl.num_programs(0)
    rows, hidden = x_hbm.shape
    ff = w1_ref.shape[2]
    piece = stage.shape[1]
    pieces = rows // piece

    @pl.when(e == 0)
    def _():
        def fetch(i, slot):
            return pltpu.make_async_copy(x_hbm.at[pl.ds(i * piece, piece), :], stage.at[slot], in_sem.at[slot])
        fetch(0, 0).start()
        for i in range(pieces):
            if i + 1 < pieces:
                fetch(i + 1, (i + 1) % 2).start()
            fetch(i, i % 2).wait()
            xf[i * piece:(i + 1) * piece, :] = stage[i % 2].astype(jnp.float32)
            yf[i * piece:(i + 1) * piece, :] = jnp.zeros((piece, hidden), jnp.float32)
        xf[rows:rows + 8, :] = jnp.zeros((8, hidden), jnp.float32)
        yf[rows:rows + 8, :] = jnp.zeros((8, hidden), jnp.float32)

    count = cnt_ref[e]

    def one_tile(i, carry):
        base = i * TILE
        groups = (jnp.minimum(count - base, TILE) + 7) // 8

        def gather(j, c):
            for r in range(8):
                tok = tok_ref[e, base + j * 8 + r]
                xg[pl.ds(j * 8 + r, 1), :] = xf[pl.ds(tok, 1), :]
            return c
        lax.fori_loop(0, groups, gather, 0)
        x = xg[...].astype(jnp.bfloat16)
        for f in range(0, ff, 256):
            g = min(f + 256, ff)
            a = jnp.dot(x, w1_ref[0, :, f:g], preferred_element_type=jnp.float32)
            b = jnp.dot(x, w3_ref[0, :, f:g], preferred_element_type=jnp.float32)
            hb[:, f:g] = (jax.nn.silu(a) * b).astype(jnp.bfloat16)
        h = hb[...]
        for d in range(0, hidden, 512):
            r = jnp.dot(h, w2_ref[0, :, d:d + 512], preferred_element_type=jnp.float32)
            rg[:, d:d + 512] = r.astype(jnp.bfloat16).astype(jnp.float32)

        def combine(j, c):
            toks = [tok_ref[e, base + j * 8 + r] for r in range(8)]
            gates = [gate_ref[e, base + j * 8 + r] for r in range(8)]
            old = [yf[pl.ds(toks[r], 1), :] for r in range(8)]
            new = [old[r] + gates[r] * rg[pl.ds(j * 8 + r, 1), :] for r in range(8)]
            for r in range(8):
                yf[pl.ds(toks[r], 1), :] = new[r]
            return c
        lax.fori_loop(0, groups, combine, 0)
        return carry

    lax.fori_loop(0, (count + TILE - 1) // TILE, one_tile, 0)

    @pl.when(e == num_e - 1)
    def _():
        copy = pltpu.make_async_copy(yf.at[pl.ds(0, rows), :], out_hbm, out_sem)
        copy.start()
        copy.wait()


def expert_ffn(cnt, tok, gate, x, w1, w3, w2):
    rows, hidden = x.shape
    num_e, _, ff = w1.shape
    piece = 128
    return pl.pallas_call(
        ffn_kernel,
        out_shape=jax.ShapeDtypeStruct((rows, hidden), jnp.float32),
        grid_spec=pltpu.PrefetchScalarGridSpec(
            num_scalar_prefetch=3,
            grid=(num_e,),
            in_specs=[pl.BlockSpec(memory_space=pl.ANY),
                      pl.BlockSpec((1, hidden, ff), lambda e, *_: (e, 0, 0)),
                      pl.BlockSpec((1, hidden, ff), lambda e, *_: (e, 0, 0)),
                      pl.BlockSpec((1, ff, hidden), lambda e, *_: (e, 0, 0))],
            out_specs=pl.BlockSpec(memory_space=pl.ANY),
            scratch_shapes=[pltpu.VMEM((2, piece, hidden), jnp.bfloat16),
                            pltpu.VMEM((rows + 8, hidden), jnp.float32),
                            pltpu.VMEM((rows + 8, hidden), jnp.float32),
                            pltpu.VMEM((TILE, hidden), jnp.float32),
                            pltpu.VMEM((TILE, ff), jnp.bfloat16),
                            pltpu.VMEM((TILE, hidden), jnp.float32),
                            pltpu.SemaphoreType.DMA((2,)),
                            pltpu.SemaphoreType.DMA],
        ),
        compiler_params=pltpu.CompilerParams(vmem_limit_bytes=VMEM_BYTES),
        cost_estimate=pl.CostEstimate(flops=6 * rows * hidden * ff, bytes_accessed=6 * num_e * hidden * ff,
                                      transcendentals=0),
        name="expert_ffn",
    )(cnt, tok, gate, x, w1, w3, w2)


def solution(mesh):
    num_ep = mesh.shape['ep']
    row_spec = P(('dp', 'ep'), None)
    replicated = P()
    expert_spec = P('ep', None, None)

    def device_step(tokens, expert_ids, gate_vals, slots, shared_w1, shared_w3, shared_w2, shared_gate, expert_w1, expert_w3, expert_w2):
        tok_count, hidden = tokens.shape
        top_k = expert_ids.shape[1]
        num_e = expert_w1.shape[0]
        num_experts = num_e * num_ep
        capacity = 8 * ((2 * tok_count * top_k + 8 * num_experts - 1) // (8 * num_experts))
        rows_max = num_ep * capacity
        sizes = chunk_sizes(tok_count)
        me = lax.axis_index('ep').astype(jnp.int32).reshape(1)

        kept_ids = jnp.where(slots >= 0, expert_ids, -1).astype(jnp.float32)
        meta = jnp.concatenate([kept_ids, gate_vals], axis=1).T
        meta = jnp.pad(meta, ((0, -meta.shape[0] % 8), (0, 0)))
        meta_all = lax.all_gather(meta, 'ep', axis=0, tiled=False)
        tok, gate, cnt = route(meta_all, me, sizes, top_k, num_e, rows_max)

        start = 0
        gathered = []
        for size in sizes:
            x = lax.all_gather(tokens[start:start + size], 'ep', axis=0, tiled=False)
            gathered.append(x.reshape(num_ep * size, hidden))
            start += size

        gate_logit = jnp.dot(tokens, shared_gate, preferred_element_type=jnp.float32)
        shared_a = jnp.dot(tokens, shared_w1, preferred_element_type=jnp.float32)
        shared_b = jnp.dot(tokens, shared_w3, preferred_element_type=jnp.float32)
        shared_h = (jax.nn.silu(shared_a) * shared_b).astype(jnp.bfloat16)
        shared_out = jnp.dot(shared_h, shared_w2, preferred_element_type=jnp.float32)
        base = tokens.astype(jnp.float32) + jax.nn.sigmoid(gate_logit)[:, None] * shared_out

        parts = []
        start = 0
        for c, size in enumerate(sizes):
            partial = expert_ffn(cnt[c], tok[c], gate[c], gathered[c], expert_w1, expert_w3, expert_w2)
            routed = lax.psum_scatter(partial.reshape(num_ep, size, hidden), 'ep', scatter_dimension=0, tiled=False)
            parts.append((base[start:start + size] + routed).astype(jnp.bfloat16))
            start += size
        return jnp.concatenate(parts, axis=0)

    return jax.shard_map(device_step, mesh=mesh, in_specs=(row_spec, row_spec, row_spec, row_spec, replicated, replicated, replicated, replicated, expert_spec, expert_spec, expert_spec), out_specs=row_spec, check_vma=False)
```

time: 917 us -> 416 us (0.45)
  Pallas kernels: 0 us -> 256 us
  blocking collectives: 280 us -> 25.3 us
  waiting for transfers between devices: 262 us -> 68.5 us
  matrix products: 192 us -> 35.1 us
  local copies, waits for them, and re-layouts: 138 us -> 14 us
  other arithmetic: 34.9 us -> 5.61 us
  between operations: 0.43 us -> 13.7 us
    all_to_all x1 -> x0, blocking collectives: 280 us -> none  [device_step(): lax.all_to_all(send_buf.reshape(num_ep, local_experts * capacity, hidden)...]
    all_to_all x1 -> x0, waiting for transfers between devices: 262 us -> none  [device_step(): lax.all_to_all(expert_out.reshape(num_ep, local_experts * capacity, hidde...]
    pallas_call x0 -> x5, Pallas kernels: none -> 256 us  [the longest x4 253 us: expert_ffn(): pl.pallas_call(ffn_kernel, out_shape=jax.ShapeDtypeStruct((rows, hidden),...]
    dot_general x3 -> x0, matrix products: 156 us -> none  [the longest x1 58.6 us: device_step(): jnp.einsum('secd,edf->secf', expert_in, expert_w1, preferred_element_type...]
    gather x3 -> x0, local copies, waits for them, and re-layouts: 104 us -> none  [the longest x2 55.6 us: device_step(): jnp.take(back_buf.reshape(buf_rows, hidden), slot_dest, axis=0, mode='fil...]
    reduce_scatter x0 -> x4, waiting for transfers between devices: none -> 66.3 us  [device_step(): lax.psum_scatter(partial.reshape(num_ep, size, hidden), 'ep', scatter_dim...]
    all_gather x0 -> x1, blocking collectives: none -> 25.3 us  [device_step(): meta_all = lax.all_gather(meta, 'ep', axis=0, tiled=False)]
    reduce_sum x1 -> x0, other arithmetic: 21.2 us -> none  [device_step(): routed = jnp.sum(weights * picked, axis=1)]
  transfers between devices with their start and end apart: 1 -> 8, of which waited for: 1 -> 1; matrix products, arithmetic and copies ran while one was open for 1% -> 10% of each run, Pallas kernels for 0% -> 61%
where the time goes in v1:
time: 416 us; the launch traced here: 420 us
  Pallas kernels  256 us (62%)
  waiting for transfers between devices  68.5 us (16%)
  matrix products  35.1 us (8%)
  blocking collectives  25.3 us (6%)
  local copies, waits for them, and re-layouts  14 us (3%)
  between operations  13.7 us (3%)
  other arithmetic  5.61 us (1%)
    pallas_call x4, Pallas kernels, expert_ffn(): pl.pallas_call(ffn_kernel, out_shape=jax.ShapeDtypeStruct((rows, hidden),...  253 us
    reduce_scatter x4, waiting for transfers between devices, device_step(): lax.psum_scatter(partial.reshape(num_ep, size, hidden), 'ep', scatter_dim...  66.3 us
    all_gather x1, blocking collectives, device_step(): meta_all = lax.all_gather(meta, 'ep', axis=0, tiled=False)  25.3 us
    dot_general x1, matrix products, device_step(): jnp.dot(shared_h, shared_w2, preferred_element_type=jnp.float32)  23.4 us
    dot_general x1, matrix products, device_step(): shared_a = jnp.dot(tokens, shared_w1, preferred_element_type=jnp.float32)  11.1 us
  transfers between devices with their start and end apart: 8, of which 1 were waited for; matrix products, arithmetic and copies ran while one was open for 10% of the time, Pallas kernels for 61%

profile of v1, /device:TPU:112, one launch (start us, length us, event | category | flops | bytes accessed | tf_op | source)
XLA Modules:
  0.0 419.6 jit_solution(344391799834390161)
XLA Ops:
  6.6 2.9 fusion.4
  9.6 0.7 all-gather.10.cloned.1.call-update
  10.4 0.7 all-gather.12.cloned.1.call-update
  11.2 0.6 all-gather.14.cloned.1.call-update
  11.9 25.3 %all-gather = f32[128,512]{1,0:T(8,128)S(1)} all-gather(f32[16,512]{1,0:T(8,128)S(1)} %pad.4), channel_id=2, replica_groups=mesh['dp'=2,'ep'=8] {'ep'}, dimensions={0}, use_global_device_ids=true | all-gather | bytes 294912 | tf_op jit(solution)/shard_map/all_gather | solution.py:212
  37.2 3.2 router.1
  40.4 0.7 fusion.6
  41.2 0.7 squeeze.47.tok_ref
  41.8 0.7 fusion.5
  42.6 0.7 squeeze.48.gate_ref
  43.3 0.7 slice_reduce_fusion.3
  44.0 61.5 %expert_ffn.7 = f32[1024,2048]{1,0:T(8,128)} custom-call(s32[8]{0:T(128)} %get-tuple-element.12.cnt_ref, s32[8,768]{1,0:T(8,128)} %squeeze.47.tok_ref, f32[8,768]{1,0:T(8,128)} %squeeze.48.gate_ref, bf16[1024,2048]{1,0:T(8,128)(2,1)} %all-gather.16.cloned.1.call-done.x_hbm, bf16[8,2048,1408]{2,1,0:T(8,128)(2,1)} %w1_ref.7, bf16[8,2048,1408]{2,1,0:T(8,128)(2,1)} %w3_ref.7, ...), custom_call_target="tpu_custom_call" | custom-call | flops 17716740096 | bytes 138412032 | tf_op jit(solution)/shard_map/expert_ffn/pallas_call | solution.py:166
  105.8 0.6 copy-done.5
  106.4 0.7 squeeze.38.tok_ref
  107.1 0.7 squeeze.39.gate_ref
  107.8 61.7 %expert_ffn.4 = f32[1024,2048]{1,0:T(8,128)} custom-call(s32[8]{0:T(128)} %get-tuple-element.11.cnt_ref, s32[8,768]{1,0:T(8,128)} %squeeze.38.tok_ref, f32[8,768]{1,0:T(8,128)} %squeeze.39.gate_ref, bf16[1024,2048]{1,0:T(8,128)(2,1)} %all-gather.10.cloned.1.call-done.x_hbm, bf16[8,2048,1408]{2,1,0:T(8,128)(2,1)} %w1_ref.7, bf16[8,2048,1408]{2,1,0:T(8,128)(2,1)} %w3_ref.7, ...), custom_call_target="tpu_custom_call" | custom-call | flops 17716740096 | bytes 138412032 | tf_op jit(solution)/shard_map/expert_ffn/pallas_call | solution.py:166
  169.7 0.7 copy-done.3
  170.4 0.7 squeeze.41.tok_ref
  171.1 0.7 squeeze.42.gate_ref
  171.8 64.8 %expert_ffn.5 = f32[1024,2048]{1,0:T(8,128)} custom-call(s32[8]{0:T(128)} %get-tuple-element.14.cnt_ref, s32[8,768]{1,0:T(8,128)} %squeeze.41.tok_ref, f32[8,768]{1,0:T(8,128)} %squeeze.42.gate_ref, bf16[1024,2048]{1,0:T(8,128)(2,1)} %all-gather.12.cloned.1.call-done.x_hbm, bf16[8,2048,1408]{2,1,0:T(8,128)(2,1)} %w1_ref.7, bf16[8,2048,1408]{2,1,0:T(8,128)(2,1)} %w3_ref.7, ...), custom_call_target="tpu_custom_call" | custom-call | flops 17716740096 | bytes 138412032 | tf_op jit(solution)/shard_map/expert_ffn/pallas_call | solution.py:166
  237.0 0.5 copy-done.1
  237.5 0.7 squeeze.44.tok_ref
  238.2 0.7 squeeze.45.gate_ref
  238.9 65.3 %expert_ffn.6 = f32[1024,2048]{1,0:T(8,128)} custom-call(s32[8]{0:T(128)} %get-tuple-element.13.cnt_ref, s32[8,768]{1,0:T(8,128)} %squeeze.44.tok_ref, f32[8,768]{1,0:T(8,128)} %squeeze.45.gate_ref, bf16[1024,2048]{1,0:T(8,128)(2,1)} %all-gather.14.cloned.1.call-done.x_hbm, bf16[8,2048,1408]{2,1,0:T(8,128)(2,1)} %w1_ref.7, bf16[8,2048,1408]{2,1,0:T(8,128)(2,1)} %w3_ref.7, ...), custom_call_target="tpu_custom_call" | custom-call | flops 17716740096 | bytes 138412032 | tf_op jit(solution)/shard_map/expert_ffn/pallas_call | solution.py:166
  304.3 0.6 copy-done.10
  304.9 0.9 copy-done
  305.8 0.6 fusion.7
  306.4 11.1 %fusion.8 = f32[512,2816]{1,0:T(8,128)} fusion(bf16[512,2048]{1,0:T(8,128)(2,1)S(1)} %copy-done, bf16[2048,2816]{1,0:T(8,128)(2,1)} %param.15), kind=kOutput, calls=%fused_computation.22 | convolution fusion | flops 5905580032 | bytes 19398656 | tf_op jit(solution)/shard_map/dot_general | solution.py:223
  317.5 23.4 %multiply_add_fusion = f32[512,2048]{1,0:T(8,128)} fusion(bf16[512,2048]{1,0:T(8,128)(2,1)S(1)} %copy-done, bf16[2816,2048]{1,0:T(8,128)(2,1)} %param.17, f32[512]{0:T(512)S(1)} %add_divide_fusion, f32[512,2816]{1,0:T(8,128)} %fusion.8, bf16[2048,2816]{1,0:T(8,128)(2,1)} %param.16), kind=kOutput, calls=%fused_computation.1 | convolution fusion | flops 11822956544 | bytes 35129344 | tf_op jit(solution)/shard_map/dot_general | solution.py:226
  340.9 66.2 %reduce-scatter.9.cloned.1.call-done = f32[1,128,2048]{2,1,0:T(8,128)} async-done(((f32[8,128,2048]{2,1,0:T(8,128)}), f32[1,128,2048]{2,1,0:T(8,128)}) %reduce-scatter.9.cloned.1.call-update) | async-done | bytes 1048592 | tf_op jit(solution)/shard_map/reduce_scatter | solution.py:233
  407.2 4.0 fusion.3
  411.2 1.6 pad_maximum_fusion
  (42 shorter events, 1.2 us)
Async XLA Ops:
  6.5 5.3 %copy-start.7 = (s32[512,6]{0,1:T(8,128)S(1)}, s32[512,6]{0,1:T(8,128)}, u32[]{:S(2)}) copy-start(s32[512,6]{0,1:T(8,128)} %param.12) | copy-start | bytes 36868
  6.5 5.3 %copy-start.8 = (s32[512,6]{0,1:T(8,128)S(1)}, s32[512,6]{0,1:T(8,128)}, u32[]{:S(2)}) copy-start(s32[512,6]{0,1:T(8,128)} %param.14) | copy-start | bytes 36868
  6.6 5.3 %copy-start.9 = (f32[512,6]{0,1:T(8,128)S(1)}, f32[512,6]{0,1:T(8,128)}, u32[]{:S(2)}) copy-start(f32[512,6]{0,1:T(8,128)} %param.13) | copy-start | bytes 36868
  6.6 37.4 %all-gather.16.cloned.1.call-start = ((), (), s32[]{:S(2)}) async-start(), calls=%async_computation.11 | async-start | bytes 4718592 | tf_op jit(solution)/shard_map/all_gather | solution.py:218
  9.5 98.2 %all-gather.10.cloned.1.call-start = ((), (), s32[]{:S(2)}) async-start(), calls=%async_computation.8 | async-start | bytes 4718592 | tf_op jit(solution)/shard_map/all_gather | solution.py:218
  10.3 161.4 %all-gather.12.cloned.1.call-start = ((), (), s32[]{:S(2)}) async-start(), calls=%async_computation.9 | async-start | bytes 4718592 | tf_op jit(solution)/shard_map/all_gather | solution.py:218
  11.1 227.8 %all-gather.14.cloned.1.call-start = ((), (), s32[]{:S(2)}) async-start(), calls=%async_computation.10 | async-start | bytes 4718592 | tf_op jit(solution)/shard_map/all_gather | solution.py:218
  11.8 329.2 %reduce-scatter.11.cloned.1.call-start = ((), (), s32[]{:S(2)}) async-start(), calls=%async_computation.7 | async-start | bytes 9437184 | tf_op jit(solution)/shard_map/reduce_scatter | solution.py:233
  105.5 0.9 copy-start.5
  105.5 1.6 copy-start.6
  105.6 235.3 %reduce-scatter.5.cloned.1.call-start = ((), (), s32[]{:S(2)}) async-start(), calls=%async_computation.4 | async-start | bytes 9437184 | tf_op jit(solution)/shard_map/reduce_scatter | solution.py:233
  169.5 0.9 copy-start.3
  169.5 1.6 copy-start.4
  169.6 171.3 %reduce-scatter.7.cloned.1.call-start = ((), (), s32[]{:S(2)}) async-start(), calls=%async_computation.5 | async-start | bytes 9437184 | tf_op jit(solution)/shard_map/reduce_scatter | solution.py:233
  236.6 0.9 copy-start.1
  236.7 1.6 copy-start.2
  236.7 170.5 %reduce-scatter.9.cloned.1.call-start = ((), (), s32[]{:S(2)}) async-start(), calls=%async_computation.6 | async-start | bytes 9437184 | tf_op jit(solution)/shard_map/reduce_scatter | solution.py:233
  304.2 0.7 copy-start.10
  304.2 1.6 copy-start
Sparse Core Ops, SparseCore 0:
  9.7 31.9 all-gather.15
  43.2 27.6 all-gather.9
  72.6 27.6 all-gather.11
  101.7 27.6 all-gather.13
  131.5 48.2 reduce-scatter.10
  182.0 67.7 reduce-scatter.4
  252.0 77.5 reduce-scatter.6
  331.9 75.2 reduce-scatter.8
